TPU v7x, 32 devices: a whole 2x2x4 slice. The times are simulated.
32 devices in a mesh: tp: 8 (over y, x, core), col: 4 (over z).
Axes of the slice: x: 2, y: 2, z: 4, core: 2. Of those that a mesh axis runs over, the one named last changes fastest.
Arguments:
- gate_in: bfloat16 [128, 53248], P('col', 'tp'), may hold values from -6 to 6
- up_in: bfloat16 [128, 53248], P('col', 'tp'), may hold values from -6 to 6
- down_weight: bfloat16 [53248, 16384], P('tp', 'col'), may hold values from -0.02734375 to 0.02734375
- residual: bfloat16 [128, 16384], P('tp', 'col'), may hold values from -30 to 30
- norm_gain: bfloat16 [16384], P('col'), may hold values from 0.5 to 1.5
Outputs:
- stream: bfloat16 [128, 16384], P('tp', 'col')
- normed: bfloat16 [128, 16384], P('tp', 'col')
All inputs are finite; a program needn't handle non-finite values.
Results may differ from a plain program's by a relative error of at most 0.0034.
Values may be sent and summed in bfloat16 or wider, within the bound.
A program may use at most 128 MiB of HBM per device.

v0:
```python
import jax
import jax.numpy as jnp
from jax import lax
from jax.sharding import PartitionSpec as P

D = 16384


def gated(gate_part, up_part):
    return (jax.nn.silu(gate_part.astype(jnp.float32)) * up_part.astype(jnp.float32)).astype(
        jnp.bfloat16
    )


def body(gate_in, up_in, down_weight, residual, norm_gain):
    local_act = gated(gate_in, up_in)
    hidden = lax.all_gather(local_act, "col", axis=0, tiled=True)
    partial_value = jnp.dot(hidden, down_weight, preferred_element_type=jnp.float32)
    branch = lax.psum_scatter(partial_value, "tp", scatter_dimension=0, tiled=True)
    summed = residual.astype(jnp.float32) + branch
    local_squares = jnp.sum(summed * summed, axis=1, keepdims=True)
    mean_square = lax.psum(local_squares, "col") / D
    scaled = summed * lax.rsqrt(mean_square + 1e-05) * norm_gain.astype(jnp.float32)[None, :]
    return (summed.astype(jnp.bfloat16), scaled.astype(jnp.bfloat16))


def solution(mesh):
    in_specs = (P("col", "tp"), P("col", "tp"), P("tp", "col"), P("tp", "col"), P("col"))
    out_specs = (P("tp", "col"), P("tp", "col"))
    return jax.shard_map(body, mesh=mesh, in_specs=in_specs, out_specs=out_specs, check_vma=False)
```

profile of v0, /device:TPU:0, one launch (start us, length us, event | category | flops | bytes accessed | tf_op | source)
XLA Modules:
  0.0 134.5 jit_solution(9100638335402482563)
XLA Ops:
  7.2 0.0 all-gather.2.cloned.1.call-start
  7.2 2.1 %fusion.4 = bf16[32,6656]{1,0:T(8,128)(2,1)} fusion(bf16[32,6656]{1,0:T(8,128)(2,1)} %param.6, bf16[32,6656]{1,0:T(8,128)(2,1)} %param.5), kind=kLoop, calls=%fused_computation.6 | loop fusion | flops 1703936 | bytes 1277952 | tf_op jit(solution)/shard_map/convert_element_type | solution.py:10
  9.4 0.0 all-gather.2.cloned.1.call-update
  9.4 0.0 reduce-scatter.2.cloned.1.call-start
  9.4 42.0 %all-gather.2.cloned.1.call-done = bf16[128,6656]{1,0:T(8,128)(2,1)} async-done(((bf16[32,6656]{1,0:T(8,128)(2,1)}), bf16[128,6656]{1,0:T(8,128)(2,1)}) %all-gather.2.cloned.1.call-update) | async-done | bytes 1703952 | tf_op jit(solution)/shard_map/all_gather | solution.py:17
  51.5 21.5 %fusion.6 = f32[128,4096]{1,0:T(8,128)} fusion(bf16[128,6656]{1,0:T(8,128)(2,1)} %all-gather.2.cloned.1.call-done, bf16[6656,4096]{1,0:T(8,128)(2,1)} %param.7), kind=kOutput, calls=%fused_computation.12 | convolution fusion | flops 6979321856 | bytes 58327040 | tf_op jit(solution)/shard_map/dot_general | solution.py:18
  73.0 0.0 copy-start.1
  73.0 0.0 copy-start
  73.0 0.0 reduce-scatter.2.cloned.1.call-update
  73.0 0.7 copy-done.1
  73.7 39.4 %reduce-scatter.2.cloned.1.call-done = f32[16,4096]{1,0:T(8,128)} async-done(((f32[128,4096]{1,0:T(8,128)}), f32[16,4096]{1,0:T(8,128)}) %reduce-scatter.2.cloned.1.call-update) | async-done | bytes 262160 | tf_op jit(solution)/shard_map/reduce_scatter | solution.py:19
  113.1 0.0 copy-done
  113.1 1.1 multiply_reduce_fusion
  114.2 11.7 %psum.7 = f32[16,1]{0,1:T(1,128)S(1)} all-reduce(f32[16,1]{0,1:T(1,128)S(1)} %bitcast.5), channel_id=1, replica_groups=mesh['tp'=8,'col'=4] {'col'}, use_global_device_ids=true, to_apply=%region_2.3 | all-reduce | flops 16 | bytes 128 | tf_op jit(solution)/shard_map/psum | solution.py:22
  125.9 1.7 %multiply_convert_fusion = (bf16[16,4096]{1,0:T(8,128)(2,1)}, bf16[16,4096]{1,0:T(8,128)(2,1)}) fusion(f32[4096]{0:T(1024)S(1)} %convert_element_type.26, f32[16]{0:T(128)S(1)} %rsqrt_bitcast_fusion, f32[16,4096]{1,0:T(8,128)} %reduce-scatter.2.cloned.1.call-done, bf16[16,4096]{1,0:T(8,128)(2,1)S(1)} %copy-done), kind=kLoop, calls=%fused_computation.7 | loop fusion | flops 393216 | bytes 671808 | tf_op jit(solution)/shard_map/convert_element_type | solution.py:24
  (2 shorter events, 0.0 us)
Async XLA Ops:
  7.2 44.3 %all-gather.2.cloned.1.call-start = ((), (), s32[]{:S(2)}) async-start(), calls=%async_computation.1 | async-start | bytes 2129920 | tf_op jit(solution)/shard_map/all_gather | solution.py:17
  9.4 103.7 %reduce-scatter.2.cloned.1.call-start = ((), (), s32[]{:S(2)}) async-start(), calls=%async_computation.2 | async-start | bytes 2359296 | tf_op jit(solution)/shard_map/reduce_scatter | solution.py:19
  73.0 0.7 copy-start.1
  73.0 40.1 %copy-start = (bf16[16,4096]{1,0:T(8,128)(2,1)S(1)}, bf16[16,4096]{1,0:T(8,128)(2,1)}, u32[]{:S(2)}) copy-start(bf16[16,4096]{1,0:T(8,128)(2,1)} %param.8) | copy-start | bytes 393220
Sparse Core Ops, SparseCore 0:
  9.5 41.8 all-gather.1
  73.1 39.9 reduce-scatter.1
where the time goes:
time: 135 us; the launch traced here: 134 us
  waiting for transfers between devices  81.5 us (60%)
  matrix products  21.5 us (16%)
  between operations  14 us (10%)
  blocking collectives  11.7 us (9%)
  other arithmetic  4.96 us (4%)
    all_gather x1, waiting for transfers between devices, body(): hidden = lax.all_gather(local_act, 'col', axis=0, tiled=True)  42 us
    reduce_scatter x1, waiting for transfers between devices, body(): lax.psum_scatter(partial_value, 'tp', scatter_dimension=0, tiled=True)  39.4 us
    dot_general x1, matrix products, body(): jnp.dot(hidden, down_weight, preferred_element_type=jnp.float32)  21.5 us
    psum x1, blocking collectives, body(): mean_square = lax.psum(local_squares, 'col') / D  11.7 us
  transfers between devices with their start and end apart: 2, of which 2 were waited for; matrix products, arithmetic and copies ran while one was open for 0% of the time, Pallas kernels for 0%

commit v1 on v0

--- a/solution.py
+++ b/solution.py
@@ -14,7 +14,12 @@
 
 def body(gate_in, up_in, down_weight, residual, norm_gain):
     local_act = gated(gate_in, up_in)
-    hidden = lax.all_gather(local_act, "col", axis=0, tiled=True)
+    ring = [local_act]
+    for hop in range(3):
+        ring.append(lax.ppermute(ring[-1], "col", [(dev, (dev + 1) % 4) for dev in range(4)]))
+    hidden = jnp.roll(
+        jnp.concatenate(ring[::-1], axis=0), (lax.axis_index("col") + 1) * ring[0].shape[0], axis=0
+    )
     partial_value = jnp.dot(hidden, down_weight, preferred_element_type=jnp.float32)
     branch = lax.psum_scatter(partial_value, "tp", scatter_dimension=0, tiled=True)
     summed = residual.astype(jnp.float32) + branch

time: 135 us -> 130 us (0.963)
  waiting for transfers between devices: 81.5 us -> 75.6 us
  starting transfers between devices: 0.08 us -> 3.15 us
    all_gather x1 -> x0, waiting for transfers between devices: 42 us -> none  [body(): hidden = lax.all_gather(local_act, 'col', axis=0, tiled=True)]
    ppermute x0 -> x3, waiting for transfers between devices: none -> 36.5 us  [body(): lax.ppermute(ring[-1], 'col', [(dev, (dev + 1) % 4) for dev in range(4)])]
    ppermute x0 -> x3, starting transfers between devices: none -> 3.11 us  [body(): lax.ppermute(ring[-1], 'col', [(dev, (dev + 1) % 4) for dev in range(4)])]
  transfers between devices with their start and end apart: 2 -> 4, of which waited for: 2 -> 4; matrix products, arithmetic and copies ran while one was open for 0% -> 0% of each run, Pallas kernels for 0% -> 0%
where the time goes in v1:
time: 130 us; the launch traced here: 129 us
  waiting for transfers between devices  75.6 us (58%)
  matrix products  20.5 us (16%)
  between operations  14.1 us (11%)
  blocking collectives  11.7 us (9%)
  other arithmetic  4.19 us (3%)
  starting transfers between devices  3.15 us (2%)
    reduce_scatter x1, waiting for transfers between devices, body(): lax.psum_scatter(partial_value, 'tp', scatter_dimension=0, tiled=True)  39 us
    ppermute x3, waiting for transfers between devices, body(): lax.ppermute(ring[-1], 'col', [(dev, (dev + 1) % 4) for dev in range(4)])  36.5 us
    dot_general x1, matrix products, body(): jnp.dot(hidden, down_weight, preferred_element_type=jnp.float32)  20.5 us
    psum x1, blocking collectives, body(): mean_square = lax.psum(local_squares, 'col') / D  11.7 us
    ppermute x3, starting transfers between devices, body(): lax.ppermute(ring[-1], 'col', [(dev, (dev + 1) % 4) for dev in range(4)])  3.11 us
  transfers between devices with their start and end apart: 4, of which 4 were waited for; matrix products, arithmetic and copies ran while one was open for 0% of the time, Pallas kernels for 0%

profile of v1, /device:TPU:0, one launch (start us, length us, event | category | flops | bytes accessed | tf_op | source)
XLA Modules:
  0.0 129.5 jit_solution(12645149262315582291)
XLA Ops:
  7.2 0.0 reduce-scatter.2.cloned.1.call-start
  7.2 1.4 %fusion.6 = bf16[32,6656]{1,0:T(8,128)(2,1)S(1)} fusion(bf16[32,6656]{1,0:T(8,128)(2,1)} %param.6, bf16[32,6656]{1,0:T(8,128)(2,1)} %param.5), kind=kLoop, calls=%fused_computation.8 | loop fusion | flops 1703936 | bytes 1277952 | tf_op jit(solution)/shard_map/convert_element_type | solution.py:10
  8.6 3.1 %collective-permute-start = (bf16[32,6656]{1,0:T(8,128)(2,1)S(1)}, bf16[32,6656]{1,0:T(8,128)(2,1)S(1)}, u32[]{:S(2)}, u32[]{:S(2)}) collective-permute-start(bf16[32,6656]{1,0:T(8,128)(2,1)S(1)} %fusion.6), channel_id=1, source_target_pairs={{0,1},{1,2},{2,3},{3,0},{4,5},{5,6},{6,7},{7,4},{8,9},{9,10},{10,1... | collective-permute-start | bytes 1277960 | tf_op jit(solution)/shard_map/ppermute | solution.py:19
  11.7 11.8 %collective-permute-done = bf16[32,6656]{1,0:T(8,128)(2,1)S(1)} collective-permute-done((bf16[32,6656]{1,0:T(8,128)(2,1)S(1)}, bf16[32,6656]{1,0:T(8,128)(2,1)S(1)}, u32[]{:S(2)}, u32[]{:S(2)}) %collective-permute-start) | collective-permute-done | bytes 426016 | tf_op jit(solution)/shard_map/ppermute | solution.py:19
  23.5 0.0 collective-permute-start.1
  23.5 12.8 %collective-permute-done.1 = bf16[32,6656]{1,0:T(8,128)(2,1)S(1)} collective-permute-done((bf16[32,6656]{1,0:T(8,128)(2,1)S(1)}, bf16[32,6656]{1,0:T(8,128)(2,1)S(1)}, u32[]{:S(2)}, u32[]{:S(2)}) %collective-permute-start.1) | collective-permute-done | bytes 426016 | tf_op jit(solution)/shard_map/ppermute | solution.py:19
  36.3 0.0 collective-permute-start.2
  36.3 11.9 %collective-permute-done.2 = bf16[32,6656]{1,0:T(8,128)(2,1)S(1)} collective-permute-done((bf16[32,6656]{1,0:T(8,128)(2,1)S(1)}, bf16[32,6656]{1,0:T(8,128)(2,1)S(1)}, u32[]{:S(2)}, u32[]{:S(2)}) %collective-permute-start.2) | collective-permute-done | bytes 426016 | tf_op jit(solution)/shard_map/ppermute | solution.py:19
  48.5 0.0 copy-start.1
  48.6 0.0 copy-start
  48.6 20.5 %fusion = f32[128,4096]{1,0:T(8,128)} fusion(bf16[6656,4096]{1,0:T(8,128)(2,1)} %param.7, bf16[256,6656]{1,0:T(8,128)(2,1)S(1)} %constant_dynamic-update-slice_fusion, s32[]{:T(128)S(6)} %select_n.14), kind=kOutput, calls=%fused_computation | convolution fusion | flops 6979321856 | bytes 58327044 | tf_op jit(solution)/shard_map/dot_general | solution.py:23
  69.1 0.0 reduce-scatter.2.cloned.1.call-update
  69.1 0.0 copy-done.1
  69.1 39.0 %reduce-scatter.2.cloned.1.call-done = f32[16,4096]{1,0:T(8,128)} async-done(((f32[128,4096]{1,0:T(8,128)}), f32[16,4096]{1,0:T(8,128)}) %reduce-scatter.2.cloned.1.call-update) | async-done | bytes 262160 | tf_op jit(solution)/shard_map/reduce_scatter | solution.py:24
  108.1 0.0 copy-done
  108.1 1.1 multiply_reduce_fusion
  109.2 11.7 %psum.7 = f32[16,1]{0,1:T(1,128)S(1)} all-reduce(f32[16,1]{0,1:T(1,128)S(1)} %bitcast.4), channel_id=1, replica_groups=mesh['tp'=8,'col'=4] {'col'}, use_global_device_ids=true, to_apply=%region_2.3 | all-reduce | flops 16 | bytes 128 | tf_op jit(solution)/shard_map/psum | solution.py:27
  120.9 1.7 %multiply_convert_fusion = (bf16[16,4096]{1,0:T(8,128)(2,1)}, bf16[16,4096]{1,0:T(8,128)(2,1)}) fusion(f32[4096]{0:T(1024)S(1)} %convert_element_type.26, f32[16]{0:T(128)S(1)} %rsqrt_bitcast_fusion, f32[16,4096]{1,0:T(8,128)} %reduce-scatter.2.cloned.1.call-done, bf16[16,4096]{1,0:T(8,128)(2,1)S(1)} %copy-done), kind=kLoop, calls=%fused_computation.9 | loop fusion | flops 393216 | bytes 671808 | tf_op jit(solution)/shard_map/convert_element_type | solution.py:29
  (10 shorter events, 0.3 us)
Async XLA Ops:
  7.2 101.0 %reduce-scatter.2.cloned.1.call-start = ((), (), s32[]{:S(2)}) async-start(), calls=%async_computation.1 | async-start | bytes 2359296 | tf_op jit(solution)/shard_map/reduce_scatter | solution.py:24
  8.6 14.9 %collective-permute-start = (bf16[32,6656]{1,0:T(8,128)(2,1)S(1)}, bf16[32,6656]{1,0:T(8,128)(2,1)S(1)}, u32[]{:S(2)}, u32[]{:S(2)}) collective-permute-start(bf16[32,6656]{1,0:T(8,128)(2,1)S(1)} %fusion.6), channel_id=1, source_target_pairs={{0,1},{1,2},{2,3},{3,0},{4,5},{5,6},{6,7},{7,4},{8,9},{9,10},{10,1... | collective-permute-start | bytes 1277960 | tf_op jit(solution)/shard_map/ppermute | solution.py:19
  23.5 12.8 %collective-permute-start.1 = (bf16[32,6656]{1,0:T(8,128)(2,1)S(1)}, bf16[32,6656]{1,0:T(8,128)(2,1)S(1)}, u32[]{:S(2)}, u32[]{:S(2)}) collective-permute-start(bf16[32,6656]{1,0:T(8,128)(2,1)S(1)} %collective-permute-done), channel_id=1, source_target_pairs={{0,1},{1,2},{2,3},{3,0},{4,5},{5,6},{6,7},{7,4},{8,9},{9,10},{10,1... | collective-permute-start | bytes 1277960 | tf_op jit(solution)/shard_map/ppermute | solution.py:19
  36.3 11.9 %collective-permute-start.2 = (bf16[32,6656]{1,0:T(8,128)(2,1)S(1)}, bf16[32,6656]{1,0:T(8,128)(2,1)S(1)}, u32[]{:S(2)}, u32[]{:S(2)}) collective-permute-start(bf16[32,6656]{1,0:T(8,128)(2,1)S(1)} %collective-permute-done.1), channel_id=1, source_target_pairs={{0,1},{1,2},{2,3},{3,0},{4,5},{5,6},{6,7},{7,4},{8,9},{9,10},{10,1... | collective-permute-start | bytes 1277960 | tf_op jit(solution)/shard_map/ppermute | solution.py:19
  48.5 20.6 %copy-start.1 = (bf16[4096]{0:T(1024)(128)(2,1)S(1)}, bf16[4096]{0:T(1024)(128)(2,1)}, u32[]{:S(2)}) copy-start(bf16[4096]{0:T(1024)(128)(2,1)} %param.9) | copy-start | bytes 24580
  48.6 59.6 %copy-start = (bf16[16,4096]{1,0:T(8,128)(2,1)S(1)}, bf16[16,4096]{1,0:T(8,128)(2,1)}, u32[]{:S(2)}) copy-start(bf16[16,4096]{1,0:T(8,128)(2,1)} %param.8) | copy-start | bytes 393220
Sparse Core Ops, SparseCore 0:
  69.2 38.8 reduce-scatter.1
